TPU v7x, 32 devices: a whole 2x2x4 slice. The times are simulated.
32 devices in a mesh: dp: 2 (over x), tp: 16 (over y, z, core).
Axes of the slice: x: 2, y: 2, z: 4, core: 2. Of those that a mesh axis runs over, the one named last changes fastest.
Arguments:
- x: bfloat16 [128, 2048], P('dp'), parts along dimension 0
- k_cache: bfloat16 [128, 4096, 16, 128], P('dp', None, 'tp'), parts along dimension 0
- v_cache: bfloat16 [128, 4096, 16, 128], P('dp', None, 'tp'), parts along dimension 0
- gain_a: bfloat16 [2048], replicated
- wq: bfloat16 [2048, 2048], P(None, 'tp')
- wo: bfloat16 [2048, 2048], P('tp')
- gain_m: bfloat16 [2048], replicated
- w_gate: bfloat16 [2048, 8192], P(None, 'tp')
- w_up: bfloat16 [2048, 8192], P(None, 'tp')
- w_down: bfloat16 [8192, 2048], P('tp')
Outputs:
- output: bfloat16 [128, 2048], P('dp'), parts along dimension 0
There are 2 independent parts. A program takes and returns all parts, laid end to end along the dimension named above; an argument that names none is the same for every part.
All inputs are finite; a program needn't handle non-finite values.
Results may differ from a plain program's by a relative error of at most 0.017.
Values are sent between devices in bfloat16 or wider.
A program may use at most 2 GiB of HBM per device.

v0:
```python
import jax
import jax.numpy as jnp
from jax import lax
from jax.sharding import PartitionSpec as P

HEAD = 128
THETA = 10000


def normed(x, gain):
    wide = x.astype(jnp.float32)
    scale = lax.rsqrt(jnp.mean(wide * wide, -1, keepdims=True) + 1e-6)
    return (wide * scale * gain.astype(jnp.float32)).astype(jnp.bfloat16)


def turned(t, place, theta):
    half = t.shape[-1] // 2
    angle = place.astype(jnp.float32)[:, None] * theta ** (-jnp.arange(half, dtype=jnp.float32) / half)
    cos, sin = jnp.cos(angle)[:, None], jnp.sin(angle)[:, None]
    a, b = t[..., :half].astype(jnp.float32), t[..., half:].astype(jnp.float32)
    return jnp.concatenate([a * cos - b * sin, b * cos + a * sin], -1).astype(jnp.bfloat16)


def matmul(a, w):
    return jnp.dot(a, w, preferred_element_type=jnp.float32).astype(jnp.bfloat16)


def einsum(form, a, b):
    return jnp.einsum(form, a.astype(jnp.float32), b.astype(jnp.float32))


def seen_by(a, wq, k_cache, v_cache, head, theta):
    batch, cache, kv_heads = k_cache.shape[:3]
    place = jnp.full((batch,), cache - 1)
    q = turned(matmul(a, wq).reshape(batch, -1, head), place, theta).reshape(batch, kv_heads, -1, head)
    scores = einsum("bgsd,bugd->bgsu", q, k_cache) * head**-0.5
    weights = jax.nn.softmax(scores, -1).astype(jnp.bfloat16)
    return einsum("bgsu,bugd->bgsd", weights, v_cache).astype(jnp.bfloat16).reshape(batch, -1)


def hidden_of(b, w_gate, w_up):
    gate = jnp.dot(b, w_gate, preferred_element_type=jnp.float32)
    up = jnp.dot(b, w_up, preferred_element_type=jnp.float32)
    return (jax.nn.silu(gate) * up).astype(jnp.bfloat16)


def solution(mesh):
    def added(t, term):
        return (t.astype(jnp.float32) + lax.psum(term.astype(jnp.bfloat16), "tp").astype(jnp.float32)).astype(jnp.bfloat16)

    def step(x, k_cache, v_cache, gain_a, wq, wo, gain_m, w_gate, w_up, w_down):
        seen = seen_by(normed(x, gain_a), wq, k_cache, v_cache, HEAD, THETA)
        h = added(x, jnp.dot(seen, wo, preferred_element_type=jnp.float32))
        return added(h, jnp.dot(hidden_of(normed(h, gain_m), w_gate, w_up), w_down, preferred_element_type=jnp.float32))

    states, cache, columns, rows_of = P("dp", None), P("dp", None, "tp", None), P(None, "tp"), P("tp", None)
    return jax.shard_map(
        step,
        mesh=mesh,
        in_specs=(states, cache, cache, P(None), columns, rows_of, P(None), columns, columns, rows_of),
        out_specs=states,
        check_vma=False,
    )
```

profile of v0, /device:TPU:0, one launch (start us, length us, event | category | flops | bytes accessed | tf_op | source)
XLA Modules:
  0.0 260.7 jit_solution(17324452728745918388)
XLA Ops:
  6.5 0.0 all-reduce.3.cloned.1.call-start
  6.6 0.8 convert_element_type.68
  7.4 1.1 fusion.9
  8.5 1.4 fusion.5
  10.0 0.1 fusion.37
  10.0 0.1 maximum_bitcast_fusion
  10.1 25.3 %fusion.2 = f32[64,1,4096]{2,1,0:T(1,128)S(1)} fusion(bf16[64,4096,1,128]{3,1,2,0:T(8,128)(2,1)} %param.11, bf16[64,128,1]{1,0,2:T(8,128)(2,1)S(1)} %maximum_bitcast_fusion), kind=kOutput, calls=%fused_computation.2 | convolution fusion | flops 67108864 | bytes 68173824 | tf_op jit(solution)/shard_map/bgsd,bugd->bgsu/dot_general | solution.py:29
  35.5 0.8 fusion.8
  36.2 0.8 fusion.7
  37.0 0.8 fusion.17
  37.9 0.0 copy-start.2
  37.9 0.0 copy-start.3
  37.9 0.0 copy-start.1
  37.9 22.7 %fusion = f32[64,1,128]{2,1,0:T(1,128)S(1)} fusion(bf16[64,4096,1,128]{3,1,2,0:T(8,128)(2,1)} %param.12, bf16[64,4096,1]{1,0,2:T(8,128)(2,1)S(1)} %fusion.17), kind=kOutput, calls=%fused_computation | convolution fusion | flops 67108864 | bytes 67665920 | tf_op jit(solution)/shard_map/bgsu,bugd->bgsd/dot_general | solution.py:29
  60.6 0.9 convolution_convert_fusion.1
  61.6 0.0 all-reduce.3.cloned.1.call-update
  61.6 0.0 all-reduce.5.cloned.1.call-start
  61.7 93.8 %all-reduce.3.cloned.1.call-done = bf16[64,2048]{1,0:T(8,128)(2,1)} async-done(((bf16[64,2048]{1,0:T(8,128)(2,1)}), bf16[64,2048]{1,0:T(8,128)(2,1)}) %all-reduce.3.cloned.1.call-update) | async-done | bytes 262160 | tf_op jit(solution)/shard_map/psum | solution.py:49
  155.4 1.1 fusion.13
  156.6 2.1 fusion.28
  158.7 3.3 %convolution_convert_fusion = bf16[64,2048]{1,0:T(8,128)(2,1)} fusion(bf16[512,2048]{1,0:T(8,128)(2,1)S(1)} %copy-done, bf16[2048,512]{1,0:T(8,128)(2,1)} %param.18, f32[64,512]{1,0:T(8,128)S(1)} %fusion.28, bf16[64,2048]{1,0:T(8,128)(2,1)S(1)} %get-tuple-element.6, f32[2048]{0:T(1024)S(1)} %convert_element_type.79, f32[64]{0:T(128)S(1)} %add_rsqrt_fusion), kind=kOutput, calls=%fused_computation.4 | convolution fusion | flops 269287424 | bytes 4858112 | tf_op jit(solution)/shard_map/dot_general | solution.py:54
  162.0 0.0 all-reduce.5.cloned.1.call-update
  162.0 90.2 %all-reduce.5.cloned.1.call-done = bf16[64,2048]{1,0:T(8,128)(2,1)} async-done(((bf16[64,2048]{1,0:T(8,128)(2,1)}), bf16[64,2048]{1,0:T(8,128)(2,1)}) %all-reduce.5.cloned.1.call-update) | async-done | bytes 262160 | tf_op jit(solution)/shard_map/psum | solution.py:49
  252.2 1.7 fusion.16
  (9 shorter events, 0.1 us)
Async XLA Ops:
  6.5 152.2 %copy-start = (bf16[512,2048]{1,0:T(8,128)(2,1)S(1)}, bf16[512,2048]{1,0:T(8,128)(2,1)}, u32[]{:S(2)}) copy-start(bf16[512,2048]{1,0:T(8,128)(2,1)} %param.19) | copy-start | bytes 6291460
  6.5 148.9 %all-reduce.3.cloned.1.call-start = ((), (), s32[]{:S(2)}) async-start(), calls=%async_computation | async-start | bytes 524288 | tf_op jit(solution)/shard_map/psum | solution.py:49
  37.9 22.8 %copy-start.2 = (bf16[128,2048]{1,0:T(8,128)(2,1)S(1)}, bf16[128,2048]{1,0:T(8,128)(2,1)}, u32[]{:S(2)}) copy-start(bf16[128,2048]{1,0:T(8,128)(2,1)} %param.15) | copy-start | bytes 1572868
  37.9 23.8 %copy-start.3 = (bf16[2048]{0:T(1024)(128)(2,1)S(1)}, bf16[2048]{0:T(1024)(128)(2,1)}, u32[]{:S(2)}) copy-start(bf16[2048]{0:T(1024)(128)(2,1)} %param.16) | copy-start | bytes 12292
  37.9 117.5 %copy-start.1 = (bf16[64,2048]{1,0:T(8,128)(2,1)S(1)}, bf16[64,2048]{1,0:T(8,128)(2,1)}, u32[]{:S(2)}) copy-start(bf16[64,2048]{1,0:T(8,128)(2,1)} %param.10) | copy-start | bytes 786436
  61.6 190.6 %all-reduce.5.cloned.1.call-start = ((), (), s32[]{:S(2)}) async-start(), calls=%async_computation.1 | async-start | bytes 524288 | tf_op jit(solution)/shard_map/psum | solution.py:49
Sparse Core Ops, SparseCore 0:
  61.7 93.6 all-reduce.2
  162.1 90.0 all-reduce.4
where the time goes:
time: 261 us
  waiting for transfers between devices  184 us (70%)
  matrix products  55.8 us (21%)
  between operations  13.5 us (5%)
  other arithmetic  7.41 us (3%)
    psum x2, waiting for transfers between devices, added(): lax.psum(term.astype(jnp.bfloat16), 'tp').astype(jnp.float32)  184 us
    dot_general x2, matrix products, einsum(): return jnp.einsum(form, a.astype(jnp.float32), b.astype(jnp.float32))  48.1 us
  transfers between devices with their start and end apart: 2, of which 2 were waited for; matrix products, arithmetic and copies ran while one was open for 0% of the time, Pallas kernels for 0%

commit v1 on v0

v1 whole, which is shorter than its diff:
```python
import functools

import jax
import jax.numpy as jnp
import numpy as np
from jax import lax
from jax.experimental import pallas as pl
from jax.experimental.pallas import tpu as pltpu
from jax.sharding import PartitionSpec as P

HEAD = 128
THETA = 10000
MESH = pl.DeviceIdType.MESH
LANES = 128
GROUP = 8
HALF = 4
DEPTH = 5
CHUNKS = ((0, 16), (16, 16), (32, 16), (48, 8), (56, 8))


def turns(place):
    half = HEAD // 2
    angle = place * float(THETA) ** (-np.arange(half, dtype=np.float64) / half)
    cos, sin = np.cos(angle), np.sin(angle)
    table = np.zeros((8, HEAD), np.float32)
    table[0] = np.concatenate([cos, cos])
    table[1] = np.concatenate([-sin, sin])
    return table


def kernel(n, x_hbm, ga_hbm, gm_hbm, cs_hbm, wq_hbm, wo_hbm, wg_hbm, wu_hbm, wd_hbm, k_hbm, v_hbm, y_hbm, *scratch):
    nc = len(CHUNKS)
    (x_v, ga_v, gm_v, cs_v, wq_v, wo_v, wg_v, wu_v, wd_v, kbuf, vbuf, q_s, attn_s), scratch = scratch[:13], scratch[13:]
    own1, send1, recv1, hall, own2, send2, recv2, ybuf = (scratch[i * nc : (i + 1) * nc] for i in range(8))
    in_sem, k_sem, v_sem, send_sem, recv_sem, out_sem = scratch[8 * nc :]
    batch, cache = k_hbm.shape[:2]
    groups = batch // GROUP
    steps = 2 * groups
    d = x_v.shape[1]
    me = lax.axis_index("tp")

    barrier = pltpu.get_barrier_semaphore()

    def greet(i, _):
        pl.semaphore_signal(barrier, inc=1, device_id={"tp": lax.rem(me + i, n)}, device_id_type=MESH)
        return _

    lax.fori_loop(1, n, greet, 0)

    def load(i, src, dst):
        return pltpu.make_async_copy(src, dst, in_sem.at[i])

    loads = [
        load(i, s, t)
        for i, (s, t) in enumerate(
            (
                (x_hbm, x_v),
                (wq_hbm, wq_v),
                (ga_hbm, ga_v),
                (cs_hbm, cs_v),
                (gm_hbm, gm_v),
                (wo_hbm, wo_v),
                (wg_hbm, wg_v),
                (wu_hbm, wu_v),
                (wd_hbm, wd_v),
            )
        )
    ]

    def k_copy(t):
        slot = lax.rem(t, DEPTH)
        return pltpu.make_async_copy(k_hbm.at[pl.ds(HALF * t, HALF)], kbuf.at[slot], k_sem.at[slot])

    def v_copy(t):
        slot = lax.rem(t, DEPTH)
        return pltpu.make_async_copy(v_hbm.at[pl.ds(HALF * t, HALF)], vbuf.at[slot], v_sem.at[slot])

    for i in range(5):
        loads[i].start()
    for t in range(DEPTH):
        k_copy(t).start()
        v_copy(t).start()
        if t == 1:
            loads[5].start()
        if t == 3:
            for i in (6, 7, 8):
                loads[i].start()

    def normed(blocks, gain_v):
        total = blocks[0] * blocks[0]
        for b in blocks[1:]:
            total = total + b * b
        scale = lax.rsqrt(jnp.sum(total, -1, keepdims=True) / d + 1e-6)
        gain = gain_v[...].astype(jnp.float32)
        return jnp.concatenate([(b * scale * gain[j : j + 1]).astype(jnp.bfloat16) for j, b in enumerate(blocks)], 1)

    for i in range(4):
        loads[i].wait()
    a = normed([x_v[:, j * LANES : (j + 1) * LANES].astype(jnp.float32) for j in range(d // LANES)], ga_v)
    q = jnp.dot(a, wq_v[...], preferred_element_type=jnp.float32).astype(jnp.bfloat16).astype(jnp.float32)
    q = q * cs_v[0:1] + pltpu.roll(q, HEAD // 2, 1) * cs_v[1:2]
    q_s[...] = q.reshape(groups, GROUP, HEAD)

    rows = lax.broadcasted_iota(jnp.int32, (GROUP, HEAD), 0)

    def half_step(g, h):
        t = 2 * g + h
        slot = lax.rem(t, DEPTH)
        tile = min(cache, 512)
        qg = q_s[g]
        q_wide = jnp.concatenate([jnp.where(rows == HALF * h + j, qg, 0.0) for j in range(HALF)], 1).astype(jnp.bfloat16)
        k_copy(t).wait()
        pieces = []
        for i in range(cache // tile):
            k = jnp.concatenate([kbuf[slot, j, i * tile : (i + 1) * tile, :] for j in range(HALF)], 1)
            pieces.append(lax.dot_general(q_wide, k, (((1,), (1,)), ((), ())), preferred_element_type=jnp.float32))
        s = jnp.concatenate(pieces, 1) * HEAD**-0.5

        @pl.when(t + DEPTH < steps)
        def _():
            k_copy(t + DEPTH).start()

        e = jnp.exp(s - jnp.max(s, -1, keepdims=True))
        w = (e * (1.0 / jnp.sum(e, -1, keepdims=True))).astype(jnp.bfloat16)
        v_copy(t).wait()
        out = None
        for i in range(cache // tile):
            v = jnp.concatenate([vbuf[slot, j, i * tile : (i + 1) * tile, :] for j in range(HALF)], 1)
            part = jnp.dot(w[:, i * tile : (i + 1) * tile], v, preferred_element_type=jnp.float32)
            out = part if out is None else out + part

        @pl.when(t + DEPTH < steps)
        def _():
            v_copy(t + DEPTH).start()

        return sum(jnp.where(rows == HALF * h + j, out[:, j * HEAD : (j + 1) * HEAD], 0.0) for j in range(HALF))

    def scatter(c, phase, send, recv):
        def body(i, _):
            j = lax.rem(me + i, n)
            pltpu.make_async_remote_copy(
                src_ref=send.at[j],
                dst_ref=recv.at[me],
                send_sem=send_sem.at[phase, c],
                recv_sem=recv_sem.at[phase, c],
                device_id={"tp": j},
                device_id_type=MESH,
            ).start()
            return _

        lax.fori_loop(1, n, body, 0)

    def wait(c, phase, sent, landed):
        copy = pltpu.make_async_remote_copy(
            src_ref=sent,
            dst_ref=landed,
            send_sem=send_sem.at[phase, c],
            recv_sem=recv_sem.at[phase, c],
            device_id={"tp": lax.rem(me + 1, n)},
            device_id_type=MESH,
        )
        return copy

    def put_term(c, term, own, send):
        for j in range(n):
            piece = term[:, j * LANES : (j + 1) * LANES]
            own[j] = piece
            send[j] = piece.astype(jnp.bfloat16)

    def total(own, recv):
        acc = own[me]
        for i in range(1, n):
            acc = acc + recv[lax.rem(me + i, n)].astype(jnp.float32)
        return acc

    def first(c):
        r0, r = CHUNKS[c]
        if c == 0:
            pl.semaphore_wait(barrier, n - 1)
            loads[5].wait()
        seen = jnp.concatenate([attn_s[i] for i in range(r0 // GROUP, (r0 + r) // GROUP)], 0).astype(jnp.bfloat16)
        put_term(c, jnp.dot(seen, wo_v[...], preferred_element_type=jnp.float32), own1[c], send1[c])
        scatter(c, 0, send1[c], recv1[c])

    def second(c):
        r0, r = CHUNKS[c]
        wait(c, 0, send1[c].at[pl.ds(0, n - 1)], recv1[c].at[pl.ds(0, n - 1)]).wait_recv()
        mine = x_v[r0 : r0 + r, pl.ds(pl.multiple_of(me * LANES, LANES), LANES)].astype(jnp.float32)
        hall[c][me] = (mine + total(own1[c], recv1[c])).astype(jnp.bfloat16)

        def body(i, _):
            pltpu.make_async_remote_copy(
                src_ref=hall[c].at[me],
                dst_ref=hall[c].at[me],
                send_sem=send_sem.at[1, c],
                recv_sem=recv_sem.at[1, c],
                device_id={"tp": lax.rem(me + i, n)},
                device_id_type=MESH,
            ).start()
            return _

        lax.fori_loop(1, n, body, 0)

    def third(c):
        wait(c, 1, hall[c].at[pl.ds(0, n - 1)], hall[c].at[pl.ds(0, n - 1)]).wait_recv()
        if c == 0:
            loads[4].wait()
            for i in (6, 7, 8):
                loads[i].wait()
        b = normed([hall[c][j].astype(jnp.float32) for j in range(n)], gm_v)
        gate = jnp.dot(b, wg_v[...], preferred_element_type=jnp.float32)
        up = jnp.dot(b, wu_v[...], preferred_element_type=jnp.float32)
        hidden = (jax.nn.silu(gate) * up).astype(jnp.bfloat16)
        put_term(c, jnp.dot(hidden, wd_v[...], preferred_element_type=jnp.float32), own2[c], send2[c])
        scatter(c, 2, send2[c], recv2[c])

    def fourth(c):
        r0, r = CHUNKS[c]
        wait(c, 2, send2[c].at[pl.ds(0, n - 1)], recv2[c].at[pl.ds(0, n - 1)]).wait_recv()
        ybuf[c][...] = (hall[c][me].astype(jnp.float32) + total(own2[c], recv2[c])).astype(jnp.bfloat16)
        block = y_hbm.at[pl.ds(r0, r), pl.ds(pl.multiple_of(me * LANES, LANES), LANES)]
        pltpu.make_async_copy(ybuf[c], block, out_sem.at[c]).start()

        def body(i, _):
            pltpu.make_async_remote_copy(
                src_ref=ybuf[c],
                dst_ref=block,
                send_sem=send_sem.at[3, c],
                recv_sem=recv_sem.at[3, c],
                device_id={"tp": lax.rem(me + i, n)},
                device_id_type=MESH,
            ).start()
            return _

        lax.fori_loop(1, n, body, 0)

    at = {
        1: [(first, 0)],
        2: [(second, 0)],
        3: [(third, 0), (first, 1)],
        4: [(fourth, 0), (second, 1)],
        5: [(third, 1), (first, 2)],
        6: [(fourth, 1), (second, 2), (first, 3)],
        7: [(third, 2), (second, 3), (first, 4)],
    }
    tail = [(third, 3), (fourth, 2), (second, 4), (fourth, 3), (third, 4), (fourth, 4)]

    def step(g, carry):
        attn_s[g] = half_step(g, 0) + half_step(g, 1)
        for when, work in at.items():

            @pl.when(g == when)
            def _():
                for stage, c in work:
                    stage(c)

        return carry

    lax.fori_loop(0, groups, step, 0)
    for stage, c in tail:
        stage(c)
    for c, (r0, r) in enumerate(CHUNKS):
        many = pl.ds(0, n - 1)
        wait(c, 0, send1[c].at[many], recv1[c].at[many]).wait_send()
        wait(c, 1, hall[c].at[many], hall[c].at[many]).wait_send()
        wait(c, 2, send2[c].at[many], recv2[c].at[many]).wait_send()
        block = y_hbm.at[pl.ds(r0, r), pl.ds(0, (n - 1) * LANES)]
        wait(c, 3, send2[c].at[many], block).wait_send()
        wait(c, 3, send2[c].at[many], block).wait_recv()
        pltpu.make_async_copy(ybuf[c], y_hbm.at[pl.ds(r0, r), pl.ds(0, LANES)], out_sem.at[c]).wait()


def solution(mesh):
    n = mesh.shape["tp"]

    def step(x, k_cache, v_cache, gain_a, wq, wo, gain_m, w_gate, w_up, w_down):
        batch, cache = k_cache.shape[:2]
        d, ff = x.shape[1], w_gate.shape[1]
        nc = len(CHUNKS)
        bf, f32 = jnp.bfloat16, jnp.float32
        per_chunk = []
        for dtype, lead in ((f32, True), (bf, True), (bf, True), (bf, True), (f32, True), (bf, True), (bf, True), (bf, False)):
            per_chunk += [pltpu.VMEM(((n,) if lead else ()) + (r, LANES), dtype) for _, r in CHUNKS]
        return pl.pallas_call(
            functools.partial(kernel, n),
            out_shape=jax.ShapeDtypeStruct(x.shape, x.dtype),
            in_specs=[pl.BlockSpec(memory_space=pl.ANY)] * 11,
            out_specs=pl.BlockSpec(memory_space=pl.ANY),
            scratch_shapes=[
                pltpu.VMEM(x.shape, bf),
                pltpu.VMEM((d // LANES, LANES), bf),
                pltpu.VMEM((d // LANES, LANES), bf),
                pltpu.VMEM((8, HEAD), f32),
                pltpu.VMEM(wq.shape, bf),
                pltpu.VMEM(wo.shape, bf),
                pltpu.VMEM(w_gate.shape, bf),
                pltpu.VMEM(w_up.shape, bf),
                pltpu.VMEM(w_down.shape, bf),
                pltpu.VMEM((DEPTH, HALF, cache, HEAD), bf),
                pltpu.VMEM((DEPTH, HALF, cache, HEAD), bf),
                pltpu.VMEM((batch // GROUP, GROUP, HEAD), f32),
                pltpu.VMEM((batch // GROUP, GROUP, HEAD), f32),
                *per_chunk,
                pltpu.SemaphoreType.DMA((9,)),
                pltpu.SemaphoreType.DMA((DEPTH,)),
                pltpu.SemaphoreType.DMA((DEPTH,)),
                pltpu.SemaphoreType.DMA((4, nc)),
                pltpu.SemaphoreType.DMA((4, nc)),
                pltpu.SemaphoreType.DMA((nc,)),
            ],
            compiler_params=pltpu.CompilerParams(
                collective_id=0, has_side_effects=True, vmem_limit_bytes=66 * 1024 * 1000
            ),
        )(
            x,
            gain_a.reshape(d // LANES, LANES),
            gain_m.reshape(d // LANES, LANES),
            jnp.asarray(turns(cache - 1)),
            wq,
            wo,
            w_gate,
            w_up,
            w_down,
            k_cache.reshape(batch, cache, HEAD),
            v_cache.reshape(batch, cache, HEAD),
        )

    states, cache, columns, rows_of = P("dp", None), P("dp", None, "tp", None), P(None, "tp"), P("tp", None)
    return jax.shard_map(
        step,
        mesh=mesh,
        in_specs=(states, cache, cache, P(None), columns, rows_of, P(None), columns, columns, rows_of),
        out_specs=states,
        check_vma=False,
    )
```

time: 261 us -> 72.9 us (0.28)
  waiting for transfers between devices: 184 us -> 0 us
  Pallas kernels: 0 us -> 71.1 us
  matrix products: 55.8 us -> 0 us
  between operations: 13.5 us -> 0.01 us
  other arithmetic: 7.41 us -> 0 us
    psum x2 -> x0, waiting for transfers between devices: 184 us -> none  [added(): lax.psum(term.astype(jnp.bfloat16), 'tp').astype(jnp.float32)]
    pallas_call x0 -> x1, Pallas kernels: none -> 71.1 us  [step(): pl.pallas_call(functools.partial(kernel, n), out_shape=jax.ShapeDtypeStru...]
    dot_general x6 -> x0, matrix products: 55.8 us -> none  [the longest x2 48.1 us: einsum(): return jnp.einsum(form, a.astype(jnp.float32), b.astype(jnp.float32))]
    convert_element_type x4 -> x0, other arithmetic: 3.38 us -> none  [the longest x1 1.71 us: added(): (t.astype(jnp.float32) + lax.psum(term.astype(jnp.bfloat16), 'tp').astype...]
    reduce_sum x3 -> x0, other arithmetic: 3.03 us -> none  [the longest x2 2.24 us: normed(): scale = lax.rsqrt(jnp.mean(wide * wide, -1, keepdims=True) + 1e-06)]
  transfers between devices with their start and end apart: 2 -> 0, of which waited for: 2 -> 0; matrix products, arithmetic and copies ran while one was open for 0% -> 0% of each run, Pallas kernels for 0% -> 0%
where the time goes in v1:
time: 72.9 us; the launch traced here: 72.8 us
  Pallas kernels  71.1 us (98%)
  local copies, waits for them, and re-layouts  1.67 us (2%)
    pallas_call x1, Pallas kernels, step(): pl.pallas_call(functools.partial(kernel, n), out_shape=jax.ShapeDtypeStru...  71.1 us
    unnamed x1, local copies, waits for them, and re-layouts  1.67 us

profile of v1, /device:TPU:0, one launch (start us, length us, event | category | flops | bytes accessed | tf_op | source)
XLA Modules:
  0.0 72.8 jit_solution(11133965938165757785)
XLA Ops:
  0.0 71.1 %shard_map.109 = bf16[64,2048]{1,0:T(8,128)(2,1)} custom-call(bf16[64,2048]{1,0:T(8,128)(2,1)} %x_hbm.1, bf16[16,128]{1,0:T(8,128)(2,1)} %bitcast.4, bf16[16,128]{1,0:T(8,128)(2,1)} %bitcast.5, f32[8,128]{1,0:T(8,128)} %constant.2.clone.cs_hbm, bf16[2048,128]{1,0:T(8,128)(2,1)} %wq_hbm.1, bf16[128,2048]{1,0:T(8,128)(2,1)} %wo_hbm.1, ...), custom_call_target="tpu_custom_call" | custom-call | tf_op jit(solution)/shard_map/pallas_call | solution.py:284
  71.1 1.7 %copy.13 = bf16[64,2048]{1,0:T(8,128)(2,1)} copy(bf16[64,2048]{1,0:T(8,128)(2,1)} %shard_map.109) | data formatting | bytes 524288

commit v2 on v1

v2 whole, which is shorter than its diff:
```python
import functools

import jax
import jax.numpy as jnp
import numpy as np
from jax import lax
from jax.experimental import pallas as pl
from jax.experimental.pallas import tpu as pltpu
from jax.sharding import PartitionSpec as P

HEAD = 128
THETA = 10000
MESH = pl.DeviceIdType.MESH
LANES = 128
GROUP = 8
HALF = 4
DEPTH = 4
CHUNKS = ((0, 24), (24, 16), (40, 16), (56, 8))
OWNERS = ((2, 4, 10, 12), (2, 4, 10, 12), (2, 4, 10, 12), (3, 5, 11, 13))


def turns(place):
    half = HEAD // 2
    angle = place * float(THETA) ** (-np.arange(half, dtype=np.float64) / half)
    cos, sin = np.cos(angle), np.sin(angle)
    table = np.zeros((8, HEAD), np.float32)
    table[0] = np.concatenate([cos, cos])
    table[1] = np.concatenate([-sin, sin])
    return table


def kernel(n, x_hbm, ga_hbm, gm_hbm, cs_hbm, wq_hbm, wo_hbm, wg_hbm, wu_hbm, wd_hbm, k_hbm, v_hbm, y_v, *scratch):
    nc = len(CHUNKS)
    (x_v, ga_v, gm_v, cs_v, wq_v, wo_v, wg_v, wu_v, wd_v, kbuf, vbuf, q_s, attn_s, w_s), scratch = scratch[:14], scratch[14:]
    own1, send1, recv1, hall, own2, send2, recv2, ybuf = (scratch[i * nc : (i + 1) * nc] for i in range(8))
    in_sem, k_sem, v_sem, send_sem, recv_sem = scratch[8 * nc :]
    batch, cache = k_hbm.shape[:2]
    groups = batch // GROUP
    steps = 2 * groups
    d = x_v.shape[1]
    me = lax.axis_index("tp")

    barrier = pltpu.get_barrier_semaphore()

    def load(i, src, dst):
        return pltpu.make_async_copy(src, dst, in_sem.at[i])

    loads = [
        load(i, s, t)
        for i, (s, t) in enumerate(
            (
                (x_hbm, x_v),
                (wq_hbm, wq_v),
                (ga_hbm, ga_v),
                (cs_hbm, cs_v),
                (gm_hbm, gm_v),
                (wo_hbm, wo_v),
                (wg_hbm, wg_v),
                (wu_hbm, wu_v),
                (wd_hbm, wd_v),
            )
        )
    ]

    def k_copy(t):
        slot = lax.rem(t, DEPTH)
        return pltpu.make_async_copy(k_hbm.at[pl.ds(HALF * t, HALF)], kbuf.at[slot], k_sem.at[slot])

    def v_copy(t):
        slot = lax.rem(t, DEPTH)
        return pltpu.make_async_copy(v_hbm.at[pl.ds(HALF * t, HALF)], vbuf.at[slot], v_sem.at[slot])

    for i in range(5):
        loads[i].start()
    for t in range(DEPTH):
        k_copy(t).start()
        v_copy(t).start()
        if t == 1:
            loads[5].start()
        if t == 3:
            for i in (6, 7, 8):
                loads[i].start()

    def greet(i, _):
        pl.semaphore_signal(barrier, inc=1, device_id={"tp": lax.rem(me + i, n)}, device_id_type=MESH)
        return _

    lax.fori_loop(1, n, greet, 0)

    def normed(blocks, gain_v):
        total = blocks[0] * blocks[0]
        for b in blocks[1:]:
            total = total + b * b
        scale = lax.rsqrt(jnp.sum(total, -1, keepdims=True) / d + 1e-6)
        gain = gain_v[...].astype(jnp.float32)
        return jnp.concatenate([(b * scale * gain[j : j + 1]).astype(jnp.bfloat16) for j, b in enumerate(blocks)], 1)

    for i in range(4):
        loads[i].wait()
    a = normed([x_v[:, j * LANES : (j + 1) * LANES].astype(jnp.float32) for j in range(d // LANES)], ga_v)
    q = jnp.dot(a, wq_v[...], preferred_element_type=jnp.float32).astype(jnp.bfloat16).astype(jnp.float32)
    q = q * cs_v[0:1] + pltpu.roll(q, HEAD // 2, 1) * cs_v[1:2]
    q_s[...] = q.reshape(groups, GROUP, HEAD)

    rows = lax.broadcasted_iota(jnp.int32, (GROUP, HEAD), 0)

    tile = min(cache, 512)

    def score(g, h):
        t = 2 * g + h
        slot = lax.rem(t, DEPTH)
        qg = q_s[g]
        q_wide = jnp.concatenate([jnp.where(rows == HALF * h + j, qg, 0.0) for j in range(HALF)], 1).astype(jnp.bfloat16)
        pieces = []
        for i in range(cache // tile):
            k = jnp.concatenate([kbuf[slot, j, i * tile : (i + 1) * tile, :] for j in range(HALF)], 1)
            pieces.append(lax.dot_general(q_wide, k, (((1,), (1,)), ((), ())), preferred_element_type=jnp.float32))
        s = jnp.concatenate(pieces, 1) * HEAD**-0.5
        e = jnp.exp(s - jnp.max(s, -1, keepdims=True))
        w_s[h] = (e * (1.0 / jnp.sum(e, -1, keepdims=True))).astype(jnp.bfloat16)

    def weigh(g, h):
        slot = lax.rem(2 * g + h, DEPTH)
        out = None
        for i in range(cache // tile):
            v = jnp.concatenate([vbuf[slot, j, i * tile : (i + 1) * tile, :] for j in range(HALF)], 1)
            part = jnp.dot(w_s[h, :, i * tile : (i + 1) * tile], v, preferred_element_type=jnp.float32)
            out = part if out is None else out + part
        return sum(jnp.where(rows == HALF * h + j, out[:, j * HEAD : (j + 1) * HEAD], 0.0) for j in range(HALF))

    def refill(copy, t):
        @pl.when(t + DEPTH < steps)
        def _():
            copy(t + DEPTH).start()

    my_y, my_z = me // 8, lax.rem(me, 8) // 2

    def place(c):
        mine = jnp.logical_and(lax.rem(me, 2) == OWNERS[c][0] % 2, jnp.logical_or(my_z == 1, my_z == 2))
        return mine, 2 * my_y + jnp.where(my_z == 2, 1, 0)

    def send(c, phase, src, dst, j):
        pltpu.make_async_remote_copy(
            src_ref=src,
            dst_ref=dst,
            send_sem=send_sem.at[phase, c],
            recv_sem=recv_sem.at[phase, c],
            device_id={"tp": j},
            device_id_type=MESH,
        ).start()

    def scatter(c, phase, src, dst):
        far = jnp.where(my_z < 2, 2, 1)
        for z in (far, 3 - far):
            for y in (1 - my_y, my_y):
                o = 8 * y + 2 * z + OWNERS[c][0] % 2

                @pl.when(me != o)
                def _():
                    send(c, phase, src.at[2 * y + z - 1], dst.at[me], o)

    def spread(c, phase, src, dst):
        core = OWNERS[c][0] % 2
        for z in (3, 2, 0, 1):
            for y in (1 - my_y, my_y):
                for other in (1 - core, core):
                    if z != 1 or y is not my_y or other != core:
                        send(c, phase, src, dst, 8 * y + 2 * (z + (my_z - 1) * (3 - 2 * z)) + other)

    def waits(c, phase, ref):
        return pltpu.make_async_remote_copy(
            src_ref=ref,
            dst_ref=ref,
            send_sem=send_sem.at[phase, c],
            recv_sem=recv_sem.at[phase, c],
            device_id={"tp": lax.rem(me + 1, n)},
            device_id_type=MESH,
        )

    def wait_pieces(c, phase, ref, sent=False):
        mine, _ = place(c)
        many = len(OWNERS[c])

        def wait(k):
            copy = waits(c, phase, ref.at[pl.ds(0, k)])
            copy.wait_send() if sent else copy.wait_recv()

        @pl.when(mine)
        def _():
            wait(many - 1)

        @pl.when(jnp.logical_not(mine))
        def _():
            wait(many)

    def put_term(c, term, own, out):
        w = d // len(OWNERS[c])
        for p in range(len(OWNERS[c])):
            piece = term[:, p * w : (p + 1) * w]
            own[p] = piece
            out[p] = piece.astype(jnp.bfloat16)

    def total(piece, own, recv):
        acc = own[piece]
        for i in range(1, n):
            acc = acc + recv[lax.rem(me + i, n)].astype(jnp.float32)
        return acc

    def first(c):
        r0, r = CHUNKS[c]
        if c == 0:
            pl.semaphore_wait(barrier, n - 1)
            loads[5].wait()
        seen = jnp.concatenate([attn_s[i] for i in range(r0 // GROUP, (r0 + r) // GROUP)], 0).astype(jnp.bfloat16)
        put_term(c, jnp.dot(seen, wo_v[...], preferred_element_type=jnp.float32), own1[c], send1[c])
        scatter(c, 0, send1[c], recv1[c])

    def second(c):
        r0, r = CHUNKS[c]
        w = d // len(OWNERS[c])
        mine, piece = place(c)

        @pl.when(mine)
        def _():
            waits(c, 0, recv1[c].at[pl.ds(0, n - 1)]).wait_recv()
            x = x_v[r0 : r0 + r, pl.ds(pl.multiple_of(piece * w, w), w)].astype(jnp.float32)
            hall[c][piece] = (x + total(piece, own1[c], recv1[c])).astype(jnp.bfloat16)
            spread(c, 1, hall[c].at[piece], hall[c].at[piece])

    def third(c):
        many = len(OWNERS[c])
        w = d // many
        wait_pieces(c, 1, hall[c])
        if c == 0:
            loads[4].wait()
            for i in (6, 7, 8):
                loads[i].wait()
        blocks = [
            hall[c][p, :, i * LANES : (i + 1) * LANES].astype(jnp.float32) for p in range(many) for i in range(w // LANES)
        ]
        b = normed(blocks, gm_v)
        gate = jnp.dot(b, wg_v[...], preferred_element_type=jnp.float32)
        up = jnp.dot(b, wu_v[...], preferred_element_type=jnp.float32)
        hidden = (jax.nn.silu(gate) * up).astype(jnp.bfloat16)
        put_term(c, jnp.dot(hidden, wd_v[...], preferred_element_type=jnp.float32), own2[c], send2[c])
        scatter(c, 2, send2[c], recv2[c])

    def block_of(c, piece):
        r0, r = CHUNKS[c]
        w = d // len(OWNERS[c])
        return y_v.at[pl.ds(r0, r), pl.ds(pl.multiple_of(piece * w, w), w)]

    def fourth(c):
        mine, piece = place(c)

        @pl.when(mine)
        def _():
            waits(c, 2, recv2[c].at[pl.ds(0, n - 1)]).wait_recv()
            ybuf[c][...] = (hall[c][piece].astype(jnp.float32) + total(piece, own2[c], recv2[c])).astype(jnp.bfloat16)
            spread(c, 3, ybuf[c], block_of(c, piece))
            block_of(c, piece)[...] = ybuf[c][...]

    at = {
        2: [(first, 0)],
        3: [(second, 0)],
        4: [(first, 1), (third, 0)],
        5: [(second, 1), (fourth, 0)],
        6: [(first, 2), (third, 1)],
    }
    tail = [(first, 3), (second, 2), (fourth, 1), (second, 3), (third, 2), (third, 3), (fourth, 2), (fourth, 3)]

    def second_half(g):
        k_copy(2 * g + 1).wait()
        v_copy(2 * g).wait()
        score(g, 1)
        attn_s[g] = weigh(g, 0)
        refill(k_copy, 2 * g + 1)
        refill(v_copy, 2 * g)

    def step(g, carry):
        second_half(g)
        k_copy(2 * g + 2).wait()
        v_copy(2 * g + 1).wait()
        score(g + 1, 0)
        attn_s[g] = attn_s[g] + weigh(g, 1)
        refill(k_copy, 2 * g + 2)
        refill(v_copy, 2 * g + 1)
        for when, work in at.items():

            @pl.when(g == when)
            def _():
                for stage, c in work:
                    stage(c)

        return carry

    k_copy(0).wait()
    score(0, 0)
    refill(k_copy, 0)
    lax.fori_loop(0, groups - 1, step, 0)
    second_half(groups - 1)
    v_copy(steps - 1).wait()
    attn_s[groups - 1] = attn_s[groups - 1] + weigh(groups - 1, 1)
    for stage, c in tail:
        stage(c)
    for c in range(nc):
        mine, _ = place(c)
        wait_pieces(c, 0, send1[c], True)
        wait_pieces(c, 2, send2[c], True)

        @pl.when(mine)
        def _():
            waits(c, 1, recv1[c].at[pl.ds(0, n - 1)]).wait_send()
            waits(c, 3, recv1[c].at[pl.ds(0, n - 1)]).wait_send()

        wait_pieces(c, 3, send1[c])


def solution(mesh):
    n = mesh.shape["tp"]

    def step(x, k_cache, v_cache, gain_a, wq, wo, gain_m, w_gate, w_up, w_down):
        batch, cache = k_cache.shape[:2]
        d, ff = x.shape[1], w_gate.shape[1]
        nc = len(CHUNKS)
        bf, f32 = jnp.bfloat16, jnp.float32
        sizes = [(len(o), r, d // len(o)) for o, (_, r) in zip(OWNERS, CHUNKS)]
        per_chunk = []
        for half in range(2):
            per_chunk += [pltpu.VMEM((k, r, w), f32) for k, r, w in sizes]
            per_chunk += [pltpu.VMEM((k, r, w), bf) for k, r, w in sizes]
            per_chunk += [pltpu.VMEM((n, r, w), bf) for _, r, w in sizes]
            per_chunk += [pltpu.VMEM((r, w) if half else (k, r, w), bf) for k, r, w in sizes]
        return pl.pallas_call(
            functools.partial(kernel, n),
            out_shape=pltpu.VMEM(x.shape, x.dtype),
            in_specs=[pl.BlockSpec(memory_space=pltpu.HBM)] * 11,
            out_specs=pl.BlockSpec(memory_space=pltpu.VMEM),
            scratch_shapes=[
                pltpu.VMEM(x.shape, bf),
                pltpu.VMEM((d // LANES, LANES), bf),
                pltpu.VMEM((d // LANES, LANES), bf),
                pltpu.VMEM((8, HEAD), f32),
                pltpu.VMEM(wq.shape, bf),
                pltpu.VMEM(wo.shape, bf),
                pltpu.VMEM(w_gate.shape, bf),
                pltpu.VMEM(w_up.shape, bf),
                pltpu.VMEM(w_down.shape, bf),
                pltpu.VMEM((DEPTH, HALF, cache, HEAD), bf),
                pltpu.VMEM((DEPTH, HALF, cache, HEAD), bf),
                pltpu.VMEM((batch // GROUP, GROUP, HEAD), f32),
                pltpu.VMEM((batch // GROUP, GROUP, HEAD), f32),
                pltpu.VMEM((2, GROUP, cache), bf),
                *per_chunk,
                pltpu.SemaphoreType.DMA((9,)),
                pltpu.SemaphoreType.DMA((DEPTH,)),
                pltpu.SemaphoreType.DMA((DEPTH,)),
                pltpu.SemaphoreType.DMA((4, nc)),
                pltpu.SemaphoreType.DMA((4, nc)),
            ],
            compiler_params=pltpu.CompilerParams(
                collective_id=0, has_side_effects=True, vmem_limit_bytes=56 * 1024 * 1024
            ),
        )(
            x,
            gain_a.reshape(d // LANES, LANES),
            gain_m.reshape(d // LANES, LANES),
            jnp.asarray(turns(cache - 1)),
            wq,
            wo,
            w_gate,
            w_up,
            w_down,
            k_cache.reshape(batch, cache, HEAD),
            v_cache.reshape(batch, cache, HEAD),
        )

    states, cache, columns, rows_of = P("dp", None), P("dp", None, "tp", None), P(None, "tp"), P("tp", None)
    return jax.shard_map(
        step,
        mesh=mesh,
        in_specs=(states, cache, cache, P(None), columns, rows_of, P(None), columns, columns, rows_of),
        out_specs=states,
        check_vma=False,
    )
```

time: 72.9 us -> 62.6 us (0.86)
  Pallas kernels: 71.1 us -> 61.8 us
  local copies, waits for them, and re-layouts: 1.67 us -> 0.71 us
    pallas_call x1, Pallas kernels: 71.1 us -> 61.8 us  [step(): pl.pallas_call(functools.partial(kernel, n), out_shape=pltpu.VMEM(x.shape...]
    unnamed x1, local copies, waits for them, and re-layouts: 1.67 us -> 0.71 us
where the time goes in v2:
time: 62.6 us; the launch traced here: 62.5 us
  Pallas kernels  61.8 us (99%)
  local copies, waits for them, and re-layouts  0.71 us (1%)
    pallas_call x1, Pallas kernels, step(): pl.pallas_call(functools.partial(kernel, n), out_shape=pltpu.VMEM(x.shape...  61.8 us

profile of v2, /device:TPU:0, one launch (start us, length us, event | category | flops | bytes accessed | tf_op | source)
XLA Modules:
  0.0 62.5 jit_solution(8712804414848835506)
XLA Ops:
  0.0 61.8 %shard_map.109 = bf16[64,2048]{1,0:T(8,128)(2,1)S(1)} custom-call(bf16[64,2048]{1,0:T(8,128)(2,1)} %x_hbm.1, bf16[16,128]{1,0:T(8,128)(2,1)} %bitcast.4, bf16[16,128]{1,0:T(8,128)(2,1)} %bitcast.5, f32[8,128]{1,0:T(8,128)} %constant.2.clone.cs_hbm, bf16[2048,128]{1,0:T(8,128)(2,1)} %wq_hbm.1, bf16[128,2048]{1,0:T(8,128)(2,1)} %wo_hbm.1, ...), custom_call_target="tpu_custom_call" | custom-call | tf_op jit(solution)/shard_map/pallas_call | solution.py:334
  61.8 0.7 %copy.13 = bf16[64,2048]{1,0:T(8,128)(2,1)} copy(bf16[64,2048]{1,0:T(8,128)(2,1)S(1)} %shard_map.109) | data formatting | bytes 524288

commit v3 on v2

--- a/solution.py
+++ b/solution.py
@@ -16,7 +16,7 @@
 HALF = 4
 DEPTH = 4
 CHUNKS = ((0, 24), (24, 16), (40, 16), (56, 8))
-OWNERS = ((2, 4, 10, 12), (2, 4, 10, 12), (2, 4, 10, 12), (3, 5, 11, 13))
+OWNERS = ((3, 5, 11, 13), (3, 5, 11, 13), (3, 5, 11, 13), (3, 5, 11, 13))
 
 
 def turns(place):
@@ -239,10 +239,15 @@
             hall[c][p, :, i * LANES : (i + 1) * LANES].astype(jnp.float32) for p in range(many) for i in range(w // LANES)
         ]
         b = normed(blocks, gm_v)
-        gate = jnp.dot(b, wg_v[...], preferred_element_type=jnp.float32)
-        up = jnp.dot(b, wu_v[...], preferred_element_type=jnp.float32)
-        hidden = (jax.nn.silu(gate) * up).astype(jnp.bfloat16)
-        put_term(c, jnp.dot(hidden, wd_v[...], preferred_element_type=jnp.float32), own2[c], send2[c])
+        half = wg_v.shape[1] // 2
+        term = None
+        for i in range(2):
+            gate = jnp.dot(b, wg_v[:, i * half : (i + 1) * half], preferred_element_type=jnp.float32)
+            up = jnp.dot(b, wu_v[:, i * half : (i + 1) * half], preferred_element_type=jnp.float32)
+            hidden = (jax.nn.silu(gate) * up).astype(jnp.bfloat16)
+            part = jnp.dot(hidden, wd_v[i * half : (i + 1) * half, :], preferred_element_type=jnp.float32)
+            term = part if term is None else term + part
+        put_term(c, term, own2[c], send2[c])
         scatter(c, 2, send2[c], recv2[c])
 
     def block_of(c, piece):
@@ -265,9 +270,9 @@
         3: [(second, 0)],
         4: [(first, 1), (third, 0)],
         5: [(second, 1), (fourth, 0)],
-        6: [(first, 2), (third, 1)],
+        6: [(first, 2)],
     }
-    tail = [(first, 3), (second, 2), (fourth, 1), (second, 3), (third, 2), (third, 3), (fourth, 2), (fourth, 3)]
+    tail = [(first, 3), (second, 2), (third, 1), (second, 3), (third, 2), (fourth, 1), (third, 3), (fourth, 2), (fourth, 3)]
 
     def second_half(g):
         k_copy(2 * g + 1).wait()

time: 62.6 us -> 62.1 us (level)
  no operation moved by 1% of the time
where the time goes in v3:
time: 62.1 us; the launch traced here: 62 us
  Pallas kernels  61.3 us (99%)
  local copies, waits for them, and re-layouts  0.71 us (1%)
    pallas_call x1, Pallas kernels, step(): pl.pallas_call(functools.partial(kernel, n), out_shape=pltpu.VMEM(x.shape...  61.3 us

profile of v3, /device:TPU:0, one launch (start us, length us, event | category | flops | bytes accessed | tf_op | source)
XLA Modules:
  0.0 62.0 jit_solution(16631289468107199471)
XLA Ops:
  0.0 61.3 %shard_map.109 = bf16[64,2048]{1,0:T(8,128)(2,1)S(1)} custom-call(bf16[64,2048]{1,0:T(8,128)(2,1)} %x_hbm.1, bf16[16,128]{1,0:T(8,128)(2,1)} %bitcast.4, bf16[16,128]{1,0:T(8,128)(2,1)} %bitcast.5, f32[8,128]{1,0:T(8,128)} %constant.2.clone.cs_hbm, bf16[2048,128]{1,0:T(8,128)(2,1)} %wq_hbm.1, bf16[128,2048]{1,0:T(8,128)(2,1)} %wo_hbm.1, ...), custom_call_target="tpu_custom_call" | custom-call | tf_op jit(solution)/shard_map/pallas_call | solution.py:339
  61.3 0.7 %copy.13 = bf16[64,2048]{1,0:T(8,128)(2,1)} copy(bf16[64,2048]{1,0:T(8,128)(2,1)S(1)} %shard_map.109) | data formatting | bytes 524288
